TPU v7x, 32 devices: a whole 2x2x4 slice. The times are simulated.
32 devices in a mesh: gx: 4 (over x, core), gy: 4 (over z), gz: 2 (over y).
Axes of the slice: x: 2, y: 2, z: 4, core: 2. Of those that a mesh axis runs over, the one named last changes fastest.
Arguments:
- velocity: float32 [3, 64, 128, 256], P(None, 'gx', 'gy', 'gz'), may hold values from -4 to 4
- plane_early: float32 [3, 128, 256], P(None, 'gy', 'gx'), may hold values from -4 to 4
- plane_late: float32 [3, 128, 256], P(None, 'gy', 'gx'), may hold values from -4 to 4
- blend: float32 [1], replicated, may hold values from 0 to 1
Outputs:
- advanced: float32 [3, 64, 128, 256], P(None, 'gx', 'gy', 'gz')
All inputs are finite; a program needn't handle non-finite values.
Results may differ from a plain program's by a relative error of at most 0.00002.
Values sent between devices are 32-bit elements; how exact they have to be, the bound alone decides.
A program may use at most 64 MiB of HBM per device.

v0:
```python
import jax
import jax.numpy as jnp
from jax import lax
from jax.sharding import PartitionSpec as P

STEPS = 4


courant = 0.08


def with_halo(x, sides, width, wrap):
    for axis, dim in sides:
        peers, length = (lax.axis_size(axis), x.shape[dim])
        up = [(i, (i + 1) % peers) for i in range(peers if wrap else peers - 1)]
        down = [(j, i) for i, j in up]
        last = lax.slice_in_dim(x, length - width, length, axis=dim)
        leading = lax.slice_in_dim(x, 0, width, axis=dim)
        before = lax.ppermute(last, axis, up)
        after = lax.ppermute(leading, axis, down)
        x = jnp.concatenate([before, x, after], axis=dim)
    return x


def advect(padded):
    center = padded[:, 1:-1, 1:-1, 1:-1]
    stream_u = center[0:1]
    span_v = center[1:2]
    vert_w = center[2:3]
    back_x = center - padded[:, :-2, 1:-1, 1:-1]
    ahead_x = padded[:, 2:, 1:-1, 1:-1] - center
    back_y = center - padded[:, 1:-1, :-2, 1:-1]
    ahead_y = padded[:, 1:-1, 2:, 1:-1] - center
    back_z = center - padded[:, 1:-1, 1:-1, :-2]
    ahead_z = padded[:, 1:-1, 1:-1, 2:] - center
    tendency = (
        jnp.maximum(stream_u, 0.0) * back_x
        + jnp.minimum(stream_u, 0.0) * ahead_x
        + (jnp.maximum(span_v, 0.0) * back_y + jnp.minimum(span_v, 0.0) * ahead_y)
        + (jnp.maximum(vert_w, 0.0) * back_z + jnp.minimum(vert_w, 0.0) * ahead_z)
    )
    return center - courant * tendency


def settle(extended, inlet_win, margin, x_first, z_first, x_total, z_total):
    x_cells = x_first - margin + jnp.arange(extended.shape[1], dtype=jnp.int32)
    z_cells = z_first - margin + jnp.arange(extended.shape[3], dtype=jnp.int32)
    inside_x = (x_cells >= 0) & (x_cells < x_total)
    inside_z = (z_cells >= 0) & (z_cells < z_total)
    at_inlet = x_cells == -1
    ghost_value = jnp.where(at_inlet[None, :, None, None], inlet_win[:, None], 0.0)
    inside = inside_x[None, :, None, None] & inside_z[None, None, None, :]
    return jnp.where(inside, extended, ghost_value)


def local(velocity, plane_early, plane_late, blend):
    weight = blend[0]
    blended = (1.0 - weight) * plane_early + weight * plane_late
    column = lax.all_gather(blended, "gx", axis=2, tiled=True)
    cells_x = velocity.shape[1]
    cells_z = velocity.shape[3]
    x_first = lax.axis_index("gx") * cells_x
    z_first = lax.axis_index("gz") * cells_z
    x_total = cells_x * lax.axis_size("gx")
    z_total = column.shape[2]
    spread = with_halo(column, (("gy", 1),), STEPS, True)
    padded_z = jnp.pad(spread, ((0, 0), (0, 0), (STEPS, STEPS)))
    inlet_full = lax.dynamic_slice_in_dim(padded_z, z_first, cells_z + 2 * STEPS, 2)
    spanned = with_halo(velocity, (("gy", 2),), STEPS, True)
    extended = with_halo(spanned, (("gx", 1), ("gz", 3)), STEPS, False)
    for substep in range(STEPS):
        margin = STEPS - substep
        inlet_win = inlet_full[
            :, substep : inlet_full.shape[1] - substep, substep : inlet_full.shape[2] - substep
        ]
        extended = settle(extended, inlet_win, margin, x_first, z_first, x_total, z_total)
        extended = advect(extended)
    return extended


def solution(mesh):
    return jax.shard_map(
        local,
        mesh=mesh,
        in_specs=(P(None, "gx", "gy", "gz"), P(None, "gy", "gx"), P(None, "gy", "gx"), P()),
        out_specs=P(None, "gx", "gy", "gz"),
        check_vma=False,
    )
```

profile of v0, /device:TPU:1, one launch (start us, length us, event | category | flops | bytes accessed | tf_op | source)
XLA Modules:
  0.0 94.3 jit_solution(7217135142423519624)
XLA Ops:
  1.7 8.5 %all_gather.3 = f32[3,32,256]{1,0,2:T(4,128)S(1)} all-gather(f32[3,32,64]{1,0,2:T(4,128)S(1)} %copy.36), channel_id=1, replica_groups=mesh['gx'=4,'gy'=4,'gz'=2] {'gx'}, dimensions={2}, use_global_device_ids=true | all-gather | bytes 122880 | tf_op jit(solution)/shard_map/all_gather | solution.py:59
  10.2 1.3 %fusion.69 = (f32[3,4,256]{1,0,2:T(4,128)}, f32[3,4,256]{1,0,2:T(4,128)}) fusion(f32[3,32,256]{1,0,2:T(4,128)S(1)} %all_gather.3), kind=kLoop, calls=%fused_computation.143 | loop fusion | bytes 49152 | tf_op jit(solution)/shard_map/slice | solution.py:18
  11.5 1.3 %collective-permute-start.6 = (f32[3,4,256]{1,0,2:T(4,128)}, f32[3,4,256]{1,0,2:T(4,128)S(1)}, u32[]{:S(2)}, u32[]{:S(2)}) collective-permute-start(f32[3,4,256]{1,0,2:T(4,128)} %get-tuple-element.36), channel_id=1, source_target_pairs={{0,2},{2,4},{4,6},{6,0},{1,3},{3,5},{5,7},{7,1},{8,10},{10,12},{12... | collective-permute-start | bytes 36872 | tf_op jit(solution)/shard_map/ppermute | solution.py:19
  12.8 2.0 %collective-permute-start.7 = (f32[3,4,256]{1,0,2:T(4,128)}, f32[3,4,256]{1,0,2:T(4,128)S(1)}, u32[]{:S(2)}, u32[]{:S(2)}) collective-permute-start(f32[3,4,256]{1,0,2:T(4,128)} %get-tuple-element.35), channel_id=1, source_target_pairs={{2,0},{4,2},{6,4},{0,6},{3,1},{5,3},{7,5},{1,7},{10,8},{12,10},{14... | collective-permute-start | bytes 36872 | tf_op jit(solution)/shard_map/ppermute | solution.py:20
  15.0 3.3 %collective-permute-start.1 = (f32[3,16,4,128]{3,1,2,0:T(8,128)S(1)}, f32[3,16,4,128]{3,1,2,0:T(8,128)S(1)}, u32[]{:S(2)}, u32[]{:S(2)}) collective-permute-start(f32[3,16,4,128]{3,1,2,0:T(8,128)S(1)} %copy.41), channel_id=1, source_target_pairs={{2,0},{4,2},{6,4},{0,6},{3,1},{5,3},{7,5},{1,7},{10,8},{12,10},{14... | collective-permute-start | bytes 294920 | tf_op jit(solution)/shard_map/ppermute | solution.py:20
  18.6 21.8 %collective-permute-done = f32[3,16,4,128]{3,1,2,0:T(8,128)S(1)} collective-permute-done((f32[3,16,4,128]{3,1,2,0:T(8,128)S(1)}, f32[3,16,4,128]{3,1,2,0:T(8,128)S(1)}, u32[]{:S(2)}, u32[]{:S(2)}) %collective-permute-start) | collective-permute-done | bytes 98336 | tf_op jit(solution)/shard_map/ppermute | solution.py:19
  40.4 1.3 %collective-permute-done.1 = f32[3,16,4,128]{3,1,2,0:T(8,128)S(1)} collective-permute-done((f32[3,16,4,128]{3,1,2,0:T(8,128)S(1)}, f32[3,16,4,128]{3,1,2,0:T(8,128)S(1)}, u32[]{:S(2)}, u32[]{:S(2)}) %collective-permute-start.1) | collective-permute-done | bytes 98336 | tf_op jit(solution)/shard_map/ppermute | solution.py:20
  42.5 3.6 %collective-permute-start.2 = (f32[3,4,40,128]{3,2,1,0:T(8,128)}, f32[3,4,40,128]{3,2,1,0:T(8,128)S(1)}, u32[]{:S(2)}, u32[]{:S(2)}) collective-permute-start(f32[3,4,40,128]{3,2,1,0:T(8,128)} %get-tuple-element.31), channel_id=1, source_target_pairs={{0,8},{8,16},{16,24},{1,9},{9,17},{17,25},{2,10},{10,18},{18,26},{... | collective-permute-start | bytes 737288 | tf_op jit(solution)/shard_map/ppermute | solution.py:19
  46.2 1.9 %collective-permute-start.3 = (f32[3,4,40,128]{3,2,1,0:T(8,128)S(1)}, f32[3,4,40,128]{3,2,1,0:T(8,128)S(1)}, u32[]{:S(2)}, u32[]{:S(2)}) collective-permute-start(f32[3,4,40,128]{3,2,1,0:T(8,128)S(1)} %get-tuple-element.32), channel_id=1, source_target_pairs={{8,0},{16,8},{24,16},{9,1},{17,9},{25,17},{10,2},{18,10},{26,18},{... | collective-permute-start | bytes 737288 | tf_op jit(solution)/shard_map/ppermute | solution.py:20
  49.6 4.1 %collective-permute-done.3 = f32[3,4,40,128]{3,2,1,0:T(8,128)S(1)} collective-permute-done((f32[3,4,40,128]{3,2,1,0:T(8,128)S(1)}, f32[3,4,40,128]{3,2,1,0:T(8,128)S(1)}, u32[]{:S(2)}, u32[]{:S(2)}) %collective-permute-start.3) | collective-permute-done | bytes 245792 | tf_op jit(solution)/shard_map/ppermute | solution.py:20
  53.9 1.6 %fusion.67 = (f32[3,24,40,4]{3,2,1,0:T(8,128)}, f32[3,24,40,4]{3,2,1,0:T(8,128)S(1)}) fusion(f32[3,24,40,128]{3,2,1,0:T(8,128)S(1)} %pad_maximum_fusion), kind=kLoop, calls=%fused_computation.141 | loop fusion | bytes 184320 | tf_op jit(solution)/shard_map/slice | solution.py:17
  55.5 2.6 %copy.42 = f32[3,24,40,4]{2,1,3,0:T(8,128)} copy(f32[3,24,40,4]{3,2,1,0:T(8,128)} %get-tuple-element.29) | data formatting | bytes 92160
  58.1 3.8 %collective-permute-start.4 = (f32[3,24,40,4]{2,1,3,0:T(8,128)}, f32[3,24,40,4]{2,1,3,0:T(8,128)}, u32[]{:S(2)}, u32[]{:S(2)}) collective-permute-start(f32[3,24,40,4]{2,1,3,0:T(8,128)} %copy.42), channel_id=1, source_target_pairs={{0,1},{2,3},{4,5},{6,7},{8,9},{10,11},{12,13},{14,15},{16,17},{18,... | collective-permute-start | bytes 138248 | tf_op jit(solution)/shard_map/ppermute | solution.py:19
  61.9 1.2 %copy.43 = f32[3,24,40,4]{2,1,3,0:T(8,128)} copy(f32[3,24,40,4]{3,2,1,0:T(8,128)S(1)} %get-tuple-element.30) | data formatting | bytes 92160
  63.1 1.5 %collective-permute-start.5 = (f32[3,24,40,4]{2,1,3,0:T(8,128)}, f32[3,24,40,4]{2,1,3,0:T(8,128)}, u32[]{:S(2)}, u32[]{:S(2)}) collective-permute-start(f32[3,24,40,4]{2,1,3,0:T(8,128)} %copy.43), channel_id=1, source_target_pairs={{1,0},{3,2},{5,4},{7,6},{9,8},{11,10},{13,12},{15,14},{17,16},{19,... | collective-permute-start | bytes 138248 | tf_op jit(solution)/shard_map/ppermute | solution.py:20
  65.1 1.5 %copy.34 = f32[3,24,40,4]{3,2,1,0:T(8,128)S(1)} copy(f32[3,24,40,4]{2,1,3,0:T(8,128)} %collective-permute-done.4) | data formatting | bytes 92160 | tf_op jit(solution)/shard_map/ppermute | solution.py:19
  66.5 2.8 %collective-permute-done.5 = f32[3,24,40,4]{2,1,3,0:T(8,128)} collective-permute-done((f32[3,24,40,4]{2,1,3,0:T(8,128)}, f32[3,24,40,4]{2,1,3,0:T(8,128)}, u32[]{:S(2)}, u32[]{:S(2)}) %collective-permute-start.5) | collective-permute-done | bytes 46112 | tf_op jit(solution)/shard_map/ppermute | solution.py:20
  69.3 2.6 %copy.35 = f32[3,24,40,4]{3,2,1,0:T(8,128)} copy(f32[3,24,40,4]{2,1,3,0:T(8,128)} %collective-permute-done.5) | data formatting | bytes 92160 | tf_op jit(solution)/shard_map/ppermute | solution.py:20
  71.9 4.6 %maximum_select_fusion = f32[3,24,40,136]{3,2,1,0:T(8,128)S(1)} fusion(f32[3,24,40,4]{3,2,1,0:T(8,128)} %copy.35, f32[3,4,40,128]{3,2,1,0:T(8,128)S(1)} %collective-permute-done.3, f32[3,16,4,128]{3,2,1,0:T(4,128)S(1)} %copy.31, f32[3,16,32,128]{3,2,1,0:T(8,128)S(1)} %copy-done, f32[3,16,4,128]{3,2,1,0:T(4,128)S(1)} %copy.30, ...), kind=kLoop, calls=%fused_computation | loop fusion | flops 3133440 | bytes 3202008 | tf_op jit(solution)/shard_map/jit(_where)/select_n | solution.py:53
  76.5 0.8 maximum_bitcast_fusion.2
  77.4 4.7 %fusion.5 = f32[3,22,38,134]{3,2,1,0:T(8,128)S(1)} fusion(f32[3,24,40,136]{3,2,1,0:T(8,128)S(1)} %maximum_select_fusion, f32[3,38,134]{2,1,0:T(8,128)S(1)} %slice.230, f32[22,38,134]{2,1,0:T(8,128)S(1)} %get-tuple-element.8, f32[22,38,134]{2,1,0:T(8,128)S(1)} %get-tuple-element.9, f32[22,38,134]{2,1,0:T(8,128)S(1)} %get-tuple-element.7, ...), kind=kLoop, calls=%fused_computation.7 | loop fusion | flops 7057512 | bytes 13506954 | tf_op jit(solution)/shard_map/jit(_where)/select_n | solution.py:53
  82.8 4.3 %fusion.19 = f32[3,20,36,132]{3,2,1,0:T(8,128)S(1)} fusion(f32[3,22,38,134]{3,2,1,0:T(8,128)S(1)} %fusion.5, f32[3,36,132]{2,1,0:T(8,128)S(1)} %slice.241, f32[20,36,132]{2,1,0:T(8,128)S(1)} %get-tuple-element.14, f32[20,36,132]{2,1,0:T(8,128)S(1)} %get-tuple-element.15, f32[20,36,132]{2,1,0:T(8,128)S(1)} %get-tuple-element.13, ...), kind=kLoop, calls=%fused_computation.27 | loop fusion | flops 5987520 | bytes 11464484 | tf_op jit(solution)/shard_map/jit(_where)/select_n | solution.py:53
  87.9 3.9 %fusion.33 = f32[3,18,34,130]{3,2,1,0:T(8,128)S(1)} fusion(f32[3,20,36,132]{3,2,1,0:T(8,128)S(1)} %fusion.19, f32[3,34,130]{2,1,0:T(8,128)S(1)} %slice.252, f32[18,34,130]{2,1,0:T(8,128)S(1)} %get-tuple-element.20, f32[18,34,130]{2,1,0:T(8,128)S(1)} %get-tuple-element.21, f32[18,34,130]{2,1,0:T(8,128)S(1)} %get-tuple-element.19, ...), kind=kLoop, calls=%fused_computation.47 | loop fusion | flops 5012280 | bytes 9602598 | tf_op jit(solution)/shard_map/jit(_where)/select_n | solution.py:53
  92.1 2.2 %fusion.46 = f32[3,16,32,128]{3,2,1,0:T(8,128)} fusion(f32[3,18,34,130]{3,2,1,0:T(8,128)S(1)} %fusion.33, f32[16,32,128]{2,1,0:T(8,128)S(1)} %get-tuple-element.26, f32[16,32,128]{2,1,0:T(8,128)S(1)} %get-tuple-element.27, f32[16,32,128]{2,1,0:T(8,128)S(1)} %get-tuple-element.25, f32[16,32,128]{2,1,0:T(8,128)S(1)} %get-tuple-element.28, ...), kind=kLoop, calls=%fused_computation.79 | loop fusion | flops 3735552 | bytes 7864320 | tf_op jit(solution)/shard_map/sub | solution.py:42
  (42 shorter events, 6.1 us)
Async XLA Ops:
  0.0 14.8 %copy-start = (f32[3,16,32,128]{3,2,1,0:T(8,128)S(1)}, f32[3,16,32,128]{3,2,1,0:T(8,128)}, u32[]{:S(2)}) copy-start(f32[3,16,32,128]{3,2,1,0:T(8,128)} %param.4) | copy-start | bytes 2359300
  11.5 37.5 %collective-permute-start.6 = (f32[3,4,256]{1,0,2:T(4,128)}, f32[3,4,256]{1,0,2:T(4,128)S(1)}, u32[]{:S(2)}, u32[]{:S(2)}) collective-permute-start(f32[3,4,256]{1,0,2:T(4,128)} %get-tuple-element.36), channel_id=1, source_target_pairs={{0,2},{2,4},{4,6},{6,0},{1,3},{3,5},{5,7},{7,1},{8,10},{10,12},{12... | collective-permute-start | bytes 36872 | tf_op jit(solution)/shard_map/ppermute | solution.py:19
  12.8 36.4 %collective-permute-start.7 = (f32[3,4,256]{1,0,2:T(4,128)}, f32[3,4,256]{1,0,2:T(4,128)S(1)}, u32[]{:S(2)}, u32[]{:S(2)}) collective-permute-start(f32[3,4,256]{1,0,2:T(4,128)} %get-tuple-element.35), channel_id=1, source_target_pairs={{2,0},{4,2},{6,4},{0,6},{3,1},{5,3},{7,5},{1,7},{10,8},{12,10},{14... | collective-permute-start | bytes 36872 | tf_op jit(solution)/shard_map/ppermute | solution.py:20
  14.9 25.5 %collective-permute-start = (f32[3,16,4,128]{3,1,2,0:T(8,128)S(1)}, f32[3,16,4,128]{3,1,2,0:T(8,128)S(1)}, u32[]{:S(2)}, u32[]{:S(2)}) collective-permute-start(f32[3,16,4,128]{3,1,2,0:T(8,128)S(1)} %copy.40), channel_id=1, source_target_pairs={{0,2},{2,4},{4,6},{6,0},{1,3},{3,5},{5,7},{7,1},{8,10},{10,12},{12... | collective-permute-start | bytes 294920 | tf_op jit(solution)/shard_map/ppermute | solution.py:19
  15.0 26.8 %collective-permute-start.1 = (f32[3,16,4,128]{3,1,2,0:T(8,128)S(1)}, f32[3,16,4,128]{3,1,2,0:T(8,128)S(1)}, u32[]{:S(2)}, u32[]{:S(2)}) collective-permute-start(f32[3,16,4,128]{3,1,2,0:T(8,128)S(1)} %copy.41), channel_id=1, source_target_pairs={{2,0},{4,2},{6,4},{0,6},{3,1},{5,3},{7,5},{1,7},{10,8},{12,10},{14... | collective-permute-start | bytes 294920 | tf_op jit(solution)/shard_map/ppermute | solution.py:20
  42.5 7.1 %collective-permute-start.2 = (f32[3,4,40,128]{3,2,1,0:T(8,128)}, f32[3,4,40,128]{3,2,1,0:T(8,128)S(1)}, u32[]{:S(2)}, u32[]{:S(2)}) collective-permute-start(f32[3,4,40,128]{3,2,1,0:T(8,128)} %get-tuple-element.31), channel_id=1, source_target_pairs={{0,8},{8,16},{16,24},{1,9},{9,17},{17,25},{2,10},{10,18},{18,26},{... | collective-permute-start | bytes 737288 | tf_op jit(solution)/shard_map/ppermute | solution.py:19
  46.2 7.5 %collective-permute-start.3 = (f32[3,4,40,128]{3,2,1,0:T(8,128)S(1)}, f32[3,4,40,128]{3,2,1,0:T(8,128)S(1)}, u32[]{:S(2)}, u32[]{:S(2)}) collective-permute-start(f32[3,4,40,128]{3,2,1,0:T(8,128)S(1)} %get-tuple-element.32), channel_id=1, source_target_pairs={{8,0},{16,8},{24,16},{9,1},{17,9},{25,17},{10,2},{18,10},{26,18},{... | collective-permute-start | bytes 737288 | tf_op jit(solution)/shard_map/ppermute | solution.py:20
  55.5 9.1 %copy-start.1 = (f32[3,32,256]{2,1,0:T(8,128)S(1)}, f32[3,32,256]{2,1,0:T(8,128)}, u32[]{:S(2)}) copy-start(f32[3,32,256]{2,1,0:T(8,128)} %copy.38) | copy-start | bytes 294916
  58.1 7.0 %collective-permute-start.4 = (f32[3,24,40,4]{2,1,3,0:T(8,128)}, f32[3,24,40,4]{2,1,3,0:T(8,128)}, u32[]{:S(2)}, u32[]{:S(2)}) collective-permute-start(f32[3,24,40,4]{2,1,3,0:T(8,128)} %copy.42), channel_id=1, source_target_pairs={{0,1},{2,3},{4,5},{6,7},{8,9},{10,11},{12,13},{14,15},{16,17},{18,... | collective-permute-start | bytes 138248 | tf_op jit(solution)/shard_map/ppermute | solution.py:19
  63.1 6.2 %collective-permute-start.5 = (f32[3,24,40,4]{2,1,3,0:T(8,128)}, f32[3,24,40,4]{2,1,3,0:T(8,128)}, u32[]{:S(2)}, u32[]{:S(2)}) collective-permute-start(f32[3,24,40,4]{2,1,3,0:T(8,128)} %copy.43), channel_id=1, source_target_pairs={{1,0},{3,2},{5,4},{7,6},{9,8},{11,10},{13,12},{15,14},{17,16},{19,... | collective-permute-start | bytes 138248 | tf_op jit(solution)/shard_map/ppermute | solution.py:20
where the time goes:
time: 94.6 us; the launch traced here: 94.3 us
  waiting for transfers between devices  30.2 us (32%)
  other arithmetic  24.6 us (26%)
  starting transfers between devices  17.5 us (18%)
  local copies, waits for them, and re-layouts  12.5 us (13%)
  blocking collectives  8.5 us (9%)
  between operations  0.97 us (1%)
    ppermute x4, waiting for transfers between devices, with_halo(): before = lax.ppermute(last, axis, up)  22 us
    select_n x4, other arithmetic, settle(): return jnp.where(inside, extended, ghost_value)  17.5 us
    ppermute x4, starting transfers between devices, with_halo(): before = lax.ppermute(last, axis, up)  8.79 us
    ppermute x4, starting transfers between devices, with_halo(): after = lax.ppermute(leading, axis, down)  8.7 us
    all_gather x1, blocking collectives, local(): column = lax.all_gather(blended, 'gx', axis=2, tiled=True)  8.5 us
    ppermute x4, waiting for transfers between devices, with_halo(): after = lax.ppermute(leading, axis, down)  8.16 us
    unnamed x8, local copies, waits for them, and re-layouts  3.88 us
    ppermute x3, local copies, waits for them, and re-layouts, with_halo(): after = lax.ppermute(leading, axis, down)  2.82 us
  transfers between devices with their start and end apart: 8, of which 5 were waited for; matrix products, arithmetic and copies ran while one was open for 6% of the time, Pallas kernels for 0%

commit v1 on v0

v1 whole, which is shorter than its diff:
```python
import functools

import jax
import jax.numpy as jnp
from jax import lax
from jax.experimental import pallas as pl
from jax.experimental.pallas import tpu as pltpu
from jax.sharding import PartitionSpec as P

STEPS = 4
COURANT = 0.08
TOP = 8

MESH = pl.DeviceIdType.MESH


def kernel(sizes, vel_hbm, early_hbm, late_hbm, blend_ref, out_ref,
           cur, early, late, inflow_send, inflow_recv,
           y_send, y_recv, z_send, z_low, z_high,
           load_sem, xs, xr, ys, yr, zs, zr, fs, fr):
    nx, ny, nz = sizes
    comps, cells_x, cells_y, cells_z = vel_hbm.shape
    share = nx // nz
    piece = early_hbm.shape[2]
    gx, gy, gz = (lax.axis_index(name) for name in ("gx", "gy", "gz"))
    own = pl.ds(TOP, cells_y)

    load_v = pltpu.make_async_copy(
        vel_hbm, cur.at[0, :, pl.ds(1, cells_x), own, :], load_sem.at[0])
    load_e = pltpu.make_async_copy(early_hbm, early, load_sem.at[1])
    load_l = pltpu.make_async_copy(late_hbm, late, load_sem.at[2])
    load_v.start()
    load_e.start()
    load_l.start()

    has_left, has_right = gx > 0, gx < nx - 1
    has_below, has_above = gz > 0, gz < nz - 1
    feeds = (gz == gx // share) & (gx != 0)
    y_up = {"gy": lax.rem(gy + 1, ny)}
    y_down = {"gy": lax.rem(gy + ny - 1, ny)}

    barrier = pltpu.get_barrier_semaphore()
    peers = [
        (has_left, {"gx": gx - 1}),
        (has_right, {"gx": gx + 1}),
        (has_below, {"gz": gz - 1}),
        (has_above, {"gz": gz + 1}),
        (feeds, {"gx": 0}),
    ]
    for k in range(share):
        source = gz * share + k
        peers.append(((gx == 0) & (source != 0), {"gx": source}))
    expected = jnp.int32(2)
    for where in (y_up, y_down):
        pl.semaphore_signal(barrier, 1, device_id=where, device_id_type=MESH)
    for present, where in peers:
        @pl.when(present)
        def _(where=where):
            pl.semaphore_signal(barrier, 1, device_id=where, device_id_type=MESH)
        expected = expected + jnp.where(present, 1, 0)

    def remote(src, dst, send, recv, where):
        return pltpu.make_async_remote_copy(
            src_ref=src, dst_ref=dst, send_sem=send, recv_sem=recv,
            device_id=where, device_id_type=MESH)

    def x_copies(t):
        return [
            (has_right, has_left, remote(
                cur.at[t, :, cells_x, own, :], cur.at[t, :, 0, own, :],
                xs.at[t, 0], xr.at[t, 0], {"gx": gx + 1})),
            (has_left, has_right, remote(
                cur.at[t, :, 1, own, :], cur.at[t, :, cells_x + 1, own, :],
                xs.at[t, 1], xr.at[t, 1], {"gx": gx - 1})),
        ]

    def y_copies(t):
        return [
            remote(y_send.at[t, 1], y_recv.at[t, 0], ys.at[t, 0], yr.at[t, 0], y_up),
            remote(y_send.at[t, 0], y_recv.at[t, 1], ys.at[t, 1], yr.at[t, 1], y_down),
        ]

    def z_copies(t):
        return [
            (has_above, has_below, remote(
                z_send.at[t], z_low.at[t], zs.at[t, 0], zr.at[t, 0], {"gz": gz + 1})),
            (has_below, has_above, remote(
                z_send.at[t], z_high.at[t], zs.at[t, 1], zr.at[t, 1], {"gz": gz - 1})),
        ]

    lane = lax.broadcasted_iota(jnp.int32, (cells_y, cells_z), 1)

    def pack(t, x, planes, acc):
        for c in range(comps):
            j = c * cells_x + x
            y_send[t, 0, j] = planes[c][0:1, :]
            y_send[t, 1, j] = planes[c][cells_y - 1:cells_y, :]
            turned = pltpu.roll(planes[c], (2 * j + 1) % cells_z, 1)
            acc = jnp.where(lane // 2 == j, turned, acc)
        return acc

    def start_x(t):
        for sends, _, copy in x_copies(t):
            pl.when(sends)(copy.start)

    def start_yz(t):
        for copy in y_copies(t):
            copy.start()
        for sends, _, copy in z_copies(t):
            pl.when(sends)(copy.start)

    for t in range(STEPS):
        @pl.when(gx == nx - 1)
        def _(t=t):
            cur[t, :, cells_x + 1, own, :] = jnp.zeros((comps, cells_y, cells_z), jnp.float32)

        @pl.when(gz == 0)
        def _(t=t):
            z_low[t] = jnp.zeros((cells_y, cells_z), jnp.float32)

        @pl.when(gz == nz - 1)
        def _(t=t):
            z_high[t] = jnp.zeros((cells_y, cells_z), jnp.float32)

    load_e.wait()
    load_l.wait()
    weight = blend_ref[0]

    def blended():
        mixed = (1.0 - weight) * early[...] + weight * late[...]
        return jnp.concatenate([mixed] * share, axis=2)

    feed = [remote(inflow_send, inflow_recv.at[k], fs.at[k], fr.at[k], {"gx": 0})
            for k in range(share)]

    @pl.when(feeds)
    def _():
        inflow_send[...] = blended()

    @pl.when((gx == 0) & (gz == 0))
    def _():
        inflow_recv[0] = blended()

    load_v.wait()
    pl.semaphore_wait(barrier, expected)
    start_x(0)

    def first(x, acc):
        return pack(0, x, [cur[0, c, x + 1, own, :] for c in range(comps)], acc)

    zero = jnp.zeros((cells_y, cells_z), jnp.float32)
    z_send[0] = lax.fori_loop(0, cells_x, first, zero)
    start_yz(0)
    for k in range(share):
        @pl.when(feeds & (lax.rem(gx, share) == k))
        def _(k=k):
            feed[k].start()

    def update(t, x, halo):
        q = [cur[t, c, x + 1, own, :] for c in range(comps)]
        ahead, back = [], []
        keep = jnp.float32(1.0)
        for c in range(comps):
            scaled = COURANT * q[c]
            back.append(jnp.maximum(scaled, 0.0))
            ahead.append(back[c] - scaled)
            keep = keep - jnp.abs(scaled)
        result = []
        for c in range(comps):
            j = c * cells_x + x
            edge = pltpu.roll(halo, lax.rem(2 * cells_z - 2 * j, cells_z), 1)
            z_prev = jnp.where(lane == 0, edge, pltpu.roll(q[c], 1, 1))
            z_next = jnp.where(lane == cells_z - 1, edge, pltpu.roll(q[c], cells_z - 1, 1))
            x_part = back[0] * cur[t, c, x, own, :] + ahead[0] * cur[t, c, x + 2, own, :]
            y_part = (back[1] * cur[t, c, x + 1, pl.ds(TOP - 1, cells_y), :]
                      + ahead[1] * cur[t, c, x + 1, pl.ds(TOP + 1, cells_y), :])
            z_part = back[2] * z_prev + ahead[2] * z_next
            result.append(keep * q[c] + (x_part + (y_part + z_part)))
        return result

    for t in range(STEPS):
        for _, recvs, copy in z_copies(t):
            pl.when(recvs)(copy.wait_recv)
        for copy in y_copies(t):
            copy.wait_recv()

        def place(x, carry, t=t):
            for c in range(comps):
                j = c * cells_x + x
                cur[t, c, x + 1, TOP - 1:TOP, :] = y_recv[t, 0, j]
                cur[t, c, x + 1, TOP + cells_y:TOP + cells_y + 1, :] = y_recv[t, 1, j]
            return carry

        lax.fori_loop(0, cells_x, place, 0)
        halo = jnp.where(lane % 2 == 0, z_low[t], pltpu.roll(z_high[t], cells_z - 2, 1))
        for _, recvs, copy in x_copies(t):
            pl.when(recvs)(copy.wait_recv)
        if t == 0:
            @pl.when(gx == 0)
            def _():
                for k in range(share):
                    @pl.when(gz * share + k != 0)
                    def _(k=k):
                        feed[k].wait_recv()
                for c in range(comps):
                    plane = inflow_recv[0, c]
                    for k in range(1, share):
                        plane = jnp.where(lane // piece == k, inflow_recv[k, c], plane)
                    for s in range(STEPS):
                        cur[s, c, 0, own, :] = plane

        if t == STEPS - 1:
            def last(x, carry, t=t, halo=halo):
                fresh = update(t, x, halo)
                for c in range(comps):
                    out_ref[c, x] = fresh[c]
                return carry

            lax.fori_loop(0, cells_x, last, 0)
        else:
            def advance(x, acc, t=t, halo=halo):
                fresh = update(t, x, halo)
                for c in range(comps):
                    cur[t + 1, c, x + 1, own, :] = fresh[c]
                return pack(t + 1, x, fresh, acc)

            acc = advance(cells_x - 1, advance(0, zero))
            start_x(t + 1)
            z_send[t + 1] = lax.fori_loop(1, cells_x - 1, advance, acc)
            start_yz(t + 1)

    for t in range(STEPS):
        for sends, _, copy in x_copies(t):
            pl.when(sends)(copy.wait_send)
        for copy in y_copies(t):
            copy.wait_send()
        for sends, _, copy in z_copies(t):
            pl.when(sends)(copy.wait_send)
    for k in range(share):
        @pl.when(feeds & (lax.rem(gx, share) == k))
        def _(k=k):
            feed[k].wait_send()


def local(sizes, velocity, plane_early, plane_late, blend):
    comps, cells_x, cells_y, cells_z = velocity.shape
    nx, ny, nz = sizes
    assert nx % nz == 0 and cells_z == 128 and 2 * comps * cells_x <= cells_z
    share = nx // nz
    planes = comps * cells_x
    block = (comps, cells_y, cells_z)
    dma = pltpu.SemaphoreType.DMA
    return pl.pallas_call(
        functools.partial(kernel, sizes),
        out_shape=jax.ShapeDtypeStruct(velocity.shape, velocity.dtype),
        in_specs=[pl.BlockSpec(memory_space=pl.ANY)] * 3
        + [pl.BlockSpec(memory_space=pltpu.SMEM)],
        out_specs=pl.BlockSpec(memory_space=pltpu.VMEM),
        scratch_shapes=[
            pltpu.VMEM((STEPS, comps, cells_x + 2, cells_y + 2 * TOP, cells_z), jnp.float32),
            pltpu.VMEM(plane_early.shape, jnp.float32),
            pltpu.VMEM(plane_late.shape, jnp.float32),
            pltpu.VMEM(block, jnp.float32),
            pltpu.VMEM((share,) + block, jnp.float32),
            pltpu.VMEM((STEPS, 2, planes, 1, cells_z), jnp.float32),
            pltpu.VMEM((STEPS, 2, planes, 1, cells_z), jnp.float32),
            pltpu.VMEM((STEPS, cells_y, cells_z), jnp.float32),
            pltpu.VMEM((STEPS, cells_y, cells_z), jnp.float32),
            pltpu.VMEM((STEPS, cells_y, cells_z), jnp.float32),
            dma((3,)),
            dma((STEPS, 2)), dma((STEPS, 2)),
            dma((STEPS, 2)), dma((STEPS, 2)),
            dma((STEPS, 2)), dma((STEPS, 2)),
            dma((share,)), dma((share,)),
        ],
        compiler_params=pltpu.CompilerParams(collective_id=0, has_side_effects=True),
        name="advect_substeps",
    )(velocity, plane_early, plane_late, blend)


def solution(mesh):
    sizes = tuple(mesh.shape[name] for name in ("gx", "gy", "gz"))
    return jax.shard_map(
        functools.partial(local, sizes),
        mesh=mesh,
        in_specs=(P(None, "gx", "gy", "gz"), P(None, "gy", "gx"), P(None, "gy", "gx"), P()),
        out_specs=P(None, "gx", "gy", "gz"),
        check_vma=False,
    )
```

time: 94.6 us -> 36.7 us (0.39)
  the two profiles are of different devices: /device:TPU:1 before, /device:TPU:0 now
where the time goes in v1:
time: 36.7 us; the launch traced here: 36.6 us
  Pallas kernels  33.8 us (92%)
  local copies, waits for them, and re-layouts  2.06 us (6%)
  between operations  0.66 us (2%)
    pallas_call x1, Pallas kernels, local(): pl.pallas_call(functools.partial(kernel, sizes), out_shape=jax.ShapeDtype...  33.8 us
    unnamed x1, local copies, waits for them, and re-layouts  2.06 us

profile of v1, /device:TPU:0, one launch (start us, length us, event | category | flops | bytes accessed | tf_op | source)
XLA Modules:
  0.0 36.6 jit_solution(7334851743319776728)
XLA Ops:
  0.7 33.8 %advect_substeps.1 = f32[3,16,32,128]{3,2,1,0:T(8,128)} custom-call(f32[3,16,32,128]{3,2,1,0:T(8,128)} %vel_hbm.1, f32[3,32,64]{2,1,0:T(8,128)} %early_hbm.1, f32[3,32,64]{2,1,0:T(8,128)} %late_hbm.1, f32[1]{0:T(128)S(6)} %copy.6.blend_ref), custom_call_target="tpu_custom_call" | custom-call | tf_op jit(solution)/shard_map/advect_substeps/pallas_call | solution.py:253
  34.5 2.1 %copy.7 = f32[3,16,32,128]{3,2,1,0:T(8,128)} copy(f32[3,16,32,128]{3,2,1,0:T(8,128)} %advect_substeps.1) | data formatting | bytes 1572864

commit v2 on v1

--- a/solution.py
+++ b/solution.py
@@ -9,6 +9,7 @@
 
 STEPS = 4
 COURANT = 0.08
+UNROLL = 7
 TOP = 8
 
 MESH = pl.DeviceIdType.MESH
@@ -109,7 +110,11 @@
         for sends, _, copy in z_copies(t):
             pl.when(sends)(copy.start)
 
+    edge_rows = jnp.zeros((comps, cells_x, 1, cells_z), jnp.float32)
     for t in range(STEPS):
+        cur[t, :, pl.ds(1, cells_x), TOP - 1:TOP, :] = edge_rows
+        cur[t, :, pl.ds(1, cells_x), TOP + cells_y:TOP + cells_y + 1, :] = edge_rows
+
         @pl.when(gx == nx - 1)
         def _(t=t):
             cur[t, :, cells_x + 1, own, :] = jnp.zeros((comps, cells_y, cells_z), jnp.float32)
@@ -149,14 +154,22 @@
         return pack(0, x, [cur[0, c, x + 1, own, :] for c in range(comps)], acc)
 
     zero = jnp.zeros((cells_y, cells_z), jnp.float32)
-    z_send[0] = lax.fori_loop(0, cells_x, first, zero)
+    z_send[0] = lax.fori_loop(0, cells_x, first, zero, unroll=UNROLL + 1)
     start_yz(0)
     for k in range(share):
         @pl.when(feeds & (lax.rem(gx, share) == k))
         def _(k=k):
             feed[k].start()
 
-    def update(t, x, halo):
+    row = lax.broadcasted_iota(jnp.int32, (TOP, cells_z), 0)
+
+    def store(t, c, x, value):
+        if t == STEPS:
+            out_ref[c, x] = value
+        else:
+            cur[t, c, x + 1, own, :] = value
+
+    def inner(t, x, left, right):
         q = [cur[t, c, x + 1, own, :] for c in range(comps)]
         ahead, back = [], []
         keep = jnp.float32(1.0)
@@ -165,33 +178,66 @@
             back.append(jnp.maximum(scaled, 0.0))
             ahead.append(back[c] - scaled)
             keep = keep - jnp.abs(scaled)
-        result = []
+        back_z = jnp.where(lane == 0, 0.0, back[2])
+        ahead_z = jnp.where(lane == cells_z - 1, 0.0, ahead[2])
+        for c in range(comps):
+            total = (back[1] * cur[t, c, x + 1, pl.ds(TOP - 1, cells_y), :]
+                     + ahead[1] * cur[t, c, x + 1, pl.ds(TOP + 1, cells_y), :])
+            total += (back_z * pltpu.roll(q[c], 1, 1)
+                      + ahead_z * pltpu.roll(q[c], cells_z - 1, 1))
+            if left:
+                total += back[0] * cur[t, c, x, own, :]
+            if right:
+                total += ahead[0] * cur[t, c, x + 2, own, :]
+            store(t + 1, c, x, keep * q[c] + total)
+
+    def inner_all(t):
+        inner(t, 0, False, True)
+
+        def body(x, carry):
+            inner(t, x, True, True)
+            return carry
+
+        lax.fori_loop(1, cells_x - 1, body, 0, unroll=UNROLL)
+        inner(t, cells_x - 1, True, False)
+
+    def finish(t, x, halo, acc, left=False, right=False):
+        scaled = COURANT * cur[t, 2, x + 1, own, :]
+        weight_z = jnp.where(
+            lane == 0, jnp.maximum(scaled, 0.0),
+            jnp.where(lane == cells_z - 1, jnp.maximum(-scaled, 0.0), 0.0))
+        first_rows = COURANT * cur[t, 1, x + 1, pl.ds(TOP, TOP), :]
+        last_rows = COURANT * cur[t, 1, x + 1, pl.ds(cells_y, TOP), :]
+        weight_first = jnp.where(row == 0, jnp.maximum(first_rows, 0.0), 0.0)
+        weight_last = jnp.where(row == TOP - 1, jnp.maximum(-last_rows, 0.0), 0.0)
+        if left:
+            weight_x = jnp.maximum(COURANT * cur[t, 0, x + 1, own, :], 0.0)
+        if right:
+            weight_x = jnp.maximum(-COURANT * cur[t, 0, x + 1, own, :], 0.0)
+        planes = []
         for c in range(comps):
             j = c * cells_x + x
-            edge = pltpu.roll(halo, lax.rem(2 * cells_z - 2 * j, cells_z), 1)
-            z_prev = jnp.where(lane == 0, edge, pltpu.roll(q[c], 1, 1))
-            z_next = jnp.where(lane == cells_z - 1, edge, pltpu.roll(q[c], cells_z - 1, 1))
-            x_part = back[0] * cur[t, c, x, own, :] + ahead[0] * cur[t, c, x + 2, own, :]
-            y_part = (back[1] * cur[t, c, x + 1, pl.ds(TOP - 1, cells_y), :]
-                      + ahead[1] * cur[t, c, x + 1, pl.ds(TOP + 1, cells_y), :])
-            z_part = back[2] * z_prev + ahead[2] * z_next
-            result.append(keep * q[c] + (x_part + (y_part + z_part)))
-        return result
+            value = out_ref[c, x] if t == STEPS - 1 else cur[t + 1, c, x + 1, own, :]
+            value += weight_z * pltpu.roll(halo, (2 * cells_z - 2 * j) % cells_z, 1)
+            if left:
+                value += weight_x * cur[t, c, x, own, :]
+            if right:
+                value += weight_x * cur[t, c, x + 2, own, :]
+            value = jnp.concatenate([
+                value[:TOP] + weight_first * y_recv[t, 0, j],
+                value[TOP:cells_y - TOP],
+                value[cells_y - TOP:] + weight_last * y_recv[t, 1, j],
+            ], axis=0)
+            store(t + 1, c, x, value)
+            planes.append(value)
+        return pack(t + 1, x, planes, acc) if t < STEPS - 1 else acc
 
     for t in range(STEPS):
+        inner_all(t)
         for _, recvs, copy in z_copies(t):
             pl.when(recvs)(copy.wait_recv)
         for copy in y_copies(t):
             copy.wait_recv()
-
-        def place(x, carry, t=t):
-            for c in range(comps):
-                j = c * cells_x + x
-                cur[t, c, x + 1, TOP - 1:TOP, :] = y_recv[t, 0, j]
-                cur[t, c, x + 1, TOP + cells_y:TOP + cells_y + 1, :] = y_recv[t, 1, j]
-            return carry
-
-        lax.fori_loop(0, cells_x, place, 0)
         halo = jnp.where(lane % 2 == 0, z_low[t], pltpu.roll(z_high[t], cells_z - 2, 1))
         for _, recvs, copy in x_copies(t):
             pl.when(recvs)(copy.wait_recv)
@@ -209,24 +255,17 @@
                     for s in range(STEPS):
                         cur[s, c, 0, own, :] = plane
 
-        if t == STEPS - 1:
-            def last(x, carry, t=t, halo=halo):
-                fresh = update(t, x, halo)
-                for c in range(comps):
-                    out_ref[c, x] = fresh[c]
-                return carry
-
-            lax.fori_loop(0, cells_x, last, 0)
-        else:
-            def advance(x, acc, t=t, halo=halo):
-                fresh = update(t, x, halo)
-                for c in range(comps):
-                    cur[t + 1, c, x + 1, own, :] = fresh[c]
-                return pack(t + 1, x, fresh, acc)
-
-            acc = advance(cells_x - 1, advance(0, zero))
+        acc = finish(t, 0, halo, zero, left=True)
+        acc = finish(t, cells_x - 1, halo, acc, right=True)
+        if t < STEPS - 1:
             start_x(t + 1)
-            z_send[t + 1] = lax.fori_loop(1, cells_x - 1, advance, acc)
+
+        def body(x, acc, t=t, halo=halo):
+            return finish(t, x, halo, acc)
+
+        acc = lax.fori_loop(1, cells_x - 1, body, acc, unroll=UNROLL)
+        if t < STEPS - 1:
+            z_send[t + 1] = acc
             start_yz(t + 1)
 
     for t in range(STEPS):
@@ -252,7 +291,7 @@
     dma = pltpu.SemaphoreType.DMA
     return pl.pallas_call(
         functools.partial(kernel, sizes),
-        out_shape=jax.ShapeDtypeStruct(velocity.shape, velocity.dtype),
+        out_shape=pltpu.VMEM(velocity.shape, velocity.dtype),
         in_specs=[pl.BlockSpec(memory_space=pl.ANY)] * 3
         + [pl.BlockSpec(memory_space=pltpu.SMEM)],
         out_specs=pl.BlockSpec(memory_space=pltpu.VMEM),

time: 36.7 us -> 26.6 us (0.72)
  Pallas kernels: 33.8 us -> 24.9 us
  local copies, waits for them, and re-layouts: 2.06 us -> 0.88 us
    pallas_call x1, Pallas kernels: 33.8 us -> 24.9 us  [local(): pl.pallas_call(functools.partial(kernel, sizes), out_shape=pltpu.VMEM(vel...]
    unnamed x1, local copies, waits for them, and re-layouts: 2.06 us -> 0.88 us
where the time goes in v2:
time: 26.6 us; the launch traced here: 26.5 us
  Pallas kernels  24.9 us (94%)
  local copies, waits for them, and re-layouts  0.88 us (3%)
  between operations  0.66 us (2%)
    pallas_call x1, Pallas kernels, local(): pl.pallas_call(functools.partial(kernel, sizes), out_shape=pltpu.VMEM(vel...  24.9 us
    unnamed x1, local copies, waits for them, and re-layouts  0.88 us

profile of v2, /device:TPU:0, one launch (start us, length us, event | category | flops | bytes accessed | tf_op | source)
XLA Modules:
  0.0 26.5 jit_solution(14545382073402028270)
XLA Ops:
  0.7 24.9 %advect_substeps.1 = f32[3,16,32,128]{3,2,1,0:T(8,128)S(1)} custom-call(f32[3,16,32,128]{3,2,1,0:T(8,128)} %vel_hbm.1, f32[3,32,64]{2,1,0:T(8,128)} %early_hbm.1, f32[3,32,64]{2,1,0:T(8,128)} %late_hbm.1, f32[1]{0:T(128)S(6)} %copy.7.blend_ref), custom_call_target="tpu_custom_call" | custom-call | tf_op jit(solution)/shard_map/advect_substeps/pallas_call | solution.py:292
  25.6 0.9 %copy.6 = f32[3,16,32,128]{3,2,1,0:T(8,128)} copy(f32[3,16,32,128]{3,2,1,0:T(8,128)S(1)} %advect_substeps.1) | data formatting | bytes 1572864

commit v3 on v2

--- a/solution.py
+++ b/solution.py
@@ -30,9 +30,9 @@
         vel_hbm, cur.at[0, :, pl.ds(1, cells_x), own, :], load_sem.at[0])
     load_e = pltpu.make_async_copy(early_hbm, early, load_sem.at[1])
     load_l = pltpu.make_async_copy(late_hbm, late, load_sem.at[2])
-    load_v.start()
     load_e.start()
     load_l.start()
+    load_v.start()
 
     has_left, has_right = gx > 0, gx < nx - 1
     has_below, has_above = gz > 0, gz < nz - 1
@@ -91,22 +91,25 @@
 
     lane = lax.broadcasted_iota(jnp.int32, (cells_y, cells_z), 1)
 
-    def pack(t, x, planes, acc):
+    def pack(x, planes, acc, rows):
         for c in range(comps):
             j = c * cells_x + x
-            y_send[t, 0, j] = planes[c][0:1, :]
-            y_send[t, 1, j] = planes[c][cells_y - 1:cells_y, :]
             turned = pltpu.roll(planes[c], (2 * j + 1) % cells_z, 1)
-            acc = jnp.where(lane // 2 == j, turned, acc)
+            acc = jnp.where(lane[rows] // 2 == j, turned, acc)
         return acc
+
+    def edge_row(t, side, c, x, value):
+        y_send[t, side, c * cells_x + x] = value
 
     def start_x(t):
         for sends, _, copy in x_copies(t):
             pl.when(sends)(copy.start)
 
-    def start_yz(t):
+    def start_y(t):
         for copy in y_copies(t):
             copy.start()
+
+    def start_z(t):
         for sends, _, copy in z_copies(t):
             pl.when(sends)(copy.start)
 
@@ -146,22 +149,31 @@
     def _():
         inflow_recv[0] = blended()
 
-    load_v.wait()
     pl.semaphore_wait(barrier, expected)
-    start_x(0)
-
-    def first(x, acc):
-        return pack(0, x, [cur[0, c, x + 1, own, :] for c in range(comps)], acc)
-
-    zero = jnp.zeros((cells_y, cells_z), jnp.float32)
-    z_send[0] = lax.fori_loop(0, cells_x, first, zero, unroll=UNROLL + 1)
-    start_yz(0)
     for k in range(share):
         @pl.when(feeds & (lax.rem(gx, share) == k))
         def _(k=k):
             feed[k].start()
 
-    row = lax.broadcasted_iota(jnp.int32, (TOP, cells_z), 0)
+    load_v.wait()
+
+    def rows_of(x, carry):
+        for c in range(comps):
+            edge_row(0, 0, c, x, cur[0, c, x + 1, TOP:TOP + 1, :])
+            edge_row(0, 1, c, x, cur[0, c, x + 1, TOP + cells_y - 1:TOP + cells_y, :])
+        return carry
+
+    lax.fori_loop(0, cells_x, rows_of, 0, unroll=UNROLL + 1)
+    start_y(0)
+    start_x(0)
+
+    def first(x, acc):
+        planes = [cur[0, c, x + 1, own, :] for c in range(comps)]
+        return pack(x, planes, acc, slice(None))
+
+    zero = jnp.zeros((cells_y, cells_z), jnp.float32)
+    z_send[0] = lax.fori_loop(0, cells_x, first, zero, unroll=UNROLL + 1)
+    start_z(0)
 
     def store(t, c, x, value):
         if t == STEPS:
@@ -201,15 +213,14 @@
         lax.fori_loop(1, cells_x - 1, body, 0, unroll=UNROLL)
         inner(t, cells_x - 1, True, False)
 
-    def finish(t, x, halo, acc, left=False, right=False):
+    middle = slice(TOP, cells_y - TOP)
+    low, high = slice(0, TOP), slice(cells_y - TOP, cells_y)
+
+    def partly(t, x, halo, acc, left=False, right=False):
         scaled = COURANT * cur[t, 2, x + 1, own, :]
         weight_z = jnp.where(
             lane == 0, jnp.maximum(scaled, 0.0),
             jnp.where(lane == cells_z - 1, jnp.maximum(-scaled, 0.0), 0.0))
-        first_rows = COURANT * cur[t, 1, x + 1, pl.ds(TOP, TOP), :]
-        last_rows = COURANT * cur[t, 1, x + 1, pl.ds(cells_y, TOP), :]
-        weight_first = jnp.where(row == 0, jnp.maximum(first_rows, 0.0), 0.0)
-        weight_last = jnp.where(row == TOP - 1, jnp.maximum(-last_rows, 0.0), 0.0)
         if left:
             weight_x = jnp.maximum(COURANT * cur[t, 0, x + 1, own, :], 0.0)
         if right:
@@ -223,22 +234,36 @@
                 value += weight_x * cur[t, c, x, own, :]
             if right:
                 value += weight_x * cur[t, c, x + 2, own, :]
-            value = jnp.concatenate([
-                value[:TOP] + weight_first * y_recv[t, 0, j],
-                value[TOP:cells_y - TOP],
-                value[cells_y - TOP:] + weight_last * y_recv[t, 1, j],
-            ], axis=0)
             store(t + 1, c, x, value)
-            planes.append(value)
-        return pack(t + 1, x, planes, acc) if t < STEPS - 1 else acc
-
+            planes.append(value[middle])
+        return pack(x, planes, acc, middle) if t < STEPS - 1 else acc
+
+    def edges(t, x, carry):
+        weights = (jnp.maximum(COURANT * cur[t, 1, x + 1, TOP:TOP + 1, :], 0.0),
+                   jnp.maximum(-COURANT * cur[t, 1, x + 1, TOP + cells_y - 1:TOP + cells_y, :], 0.0))
+        for c in range(comps):
+            for side, y in enumerate((0, cells_y - 1)):
+                term = weights[side] * y_recv[t, side, c * cells_x + x]
+                if t == STEPS - 1:
+                    out_ref[c, x, y:y + 1, :] += term
+                else:
+                    value = cur[t + 1, c, x + 1, TOP + y:TOP + y + 1, :] + term
+                    cur[t + 1, c, x + 1, TOP + y:TOP + y + 1, :] = value
+                    edge_row(t + 1, side, c, x, value)
+        return carry
+
+    some = jnp.zeros((cells_y - 2 * TOP, cells_z), jnp.float32)
+    few = jnp.zeros((TOP, cells_z), jnp.float32)
     for t in range(STEPS):
         inner_all(t)
         for _, recvs, copy in z_copies(t):
             pl.when(recvs)(copy.wait_recv)
-        for copy in y_copies(t):
-            copy.wait_recv()
         halo = jnp.where(lane % 2 == 0, z_low[t], pltpu.roll(z_high[t], cells_z - 2, 1))
+
+        def body(x, acc, t=t, halo=halo):
+            return partly(t, x, halo, acc)
+
+        acc = lax.fori_loop(1, cells_x - 1, body, some, unroll=UNROLL)
         for _, recvs, copy in x_copies(t):
             pl.when(recvs)(copy.wait_recv)
         if t == 0:
@@ -255,18 +280,27 @@
                     for s in range(STEPS):
                         cur[s, c, 0, own, :] = plane
 
-        acc = finish(t, 0, halo, zero, left=True)
-        acc = finish(t, cells_x - 1, halo, acc, right=True)
+        acc = partly(t, 0, halo, acc, left=True)
+        acc = partly(t, cells_x - 1, halo, acc, right=True)
+        for copy in y_copies(t):
+            copy.wait_recv()
+
+        def rows(x, carry, t=t):
+            return edges(t, x, carry)
+
+        lax.fori_loop(0, cells_x, rows, 0, unroll=UNROLL + 1)
         if t < STEPS - 1:
+            start_y(t + 1)
             start_x(t + 1)
 
-        def body(x, acc, t=t, halo=halo):
-            return finish(t, x, halo, acc)
-
-        acc = lax.fori_loop(1, cells_x - 1, body, acc, unroll=UNROLL)
-        if t < STEPS - 1:
-            z_send[t + 1] = acc
-            start_yz(t + 1)
+            def ends(x, accs, t=t):
+                top = [cur[t + 1, c, x + 1, pl.ds(TOP, TOP), :] for c in range(comps)]
+                last = [cur[t + 1, c, x + 1, pl.ds(cells_y, TOP), :] for c in range(comps)]
+                return pack(x, top, accs[0], low), pack(x, last, accs[1], high)
+
+            top, last = lax.fori_loop(0, cells_x, ends, (few, few), unroll=UNROLL + 1)
+            z_send[t + 1] = jnp.concatenate([top, acc, last], axis=0)
+            start_z(t + 1)
 
     for t in range(STEPS):
         for sends, _, copy in x_copies(t):

time: 26.6 us -> 23.5 us (0.88)
  Pallas kernels: 24.9 us -> 21.8 us
    pallas_call x1, Pallas kernels: 24.9 us -> 21.8 us  [local(): pl.pallas_call(functools.partial(kernel, sizes), out_shape=pltpu.VMEM(vel...]
where the time goes in v3:
time: 23.5 us; the launch traced here: 23.4 us
  Pallas kernels  21.8 us (93%)
  local copies, waits for them, and re-layouts  0.88 us (4%)
  between operations  0.66 us (3%)
    pallas_call x1, Pallas kernels, local(): pl.pallas_call(functools.partial(kernel, sizes), out_shape=pltpu.VMEM(vel...  21.8 us
    unnamed x1, local copies, waits for them, and re-layouts  0.88 us

profile of v3, /device:TPU:0, one launch (start us, length us, event | category | flops | bytes accessed | tf_op | source)
XLA Modules:
  0.0 23.4 jit_solution(3659305190805071168)
XLA Ops:
  0.7 21.8 %advect_substeps.1 = f32[3,16,32,128]{3,2,1,0:T(8,128)S(1)} custom-call(f32[3,16,32,128]{3,2,1,0:T(8,128)} %vel_hbm.1, f32[3,32,64]{2,1,0:T(8,128)} %early_hbm.1, f32[3,32,64]{2,1,0:T(8,128)} %late_hbm.1, f32[1]{0:T(128)S(6)} %copy.7.blend_ref), custom_call_target="tpu_custom_call" | custom-call | tf_op jit(solution)/shard_map/advect_substeps/pallas_call | solution.py:326
  22.5 0.9 %copy.6 = f32[3,16,32,128]{3,2,1,0:T(8,128)} copy(f32[3,16,32,128]{3,2,1,0:T(8,128)S(1)} %advect_substeps.1) | data formatting | bytes 1572864
